TPU v7x, 32 devices: a whole 2x2x4 slice. The times are simulated.
32 devices in a mesh: rep: 4 (over y, x), fsdp: 8 (over z, core).
Axes of the slice: x: 2, y: 2, z: 4, core: 2. Of those that a mesh axis runs over, the one named last changes fastest.
Arguments:
- momentum: float32 [4, 18432, 2304], P('rep', 'fsdp'), may hold values from -60 to 60
- gradient: bfloat16 [4, 18432, 2304], P('rep', 'fsdp'), may hold values from -30 to 30
- right_factor: float32 [2304, 256], P('fsdp'), may hold values from -0.125 to 0.125
Outputs:
- new_momentum: float32 [4, 18432, 2304], P('rep', 'fsdp')
- update: bfloat16 [18432, 2304], P('fsdp')
- new_factor: float32 [2304, 256], P('fsdp')
All inputs are finite; a program needn't handle non-finite values.
Results may differ from a plain program's by a relative error of at most 0.001.
Values sent between devices are 32-bit elements; how exact they have to be, the bound alone decides.
A program may use at most 128 MiB of HBM per device.

v0:
```python
import math
import jax
import jax.numpy as jnp
from jax import lax
from jax.sharding import PartitionSpec as P

ROWS = 18432
COLS = 2304
RANK = 256
epsilon = 1e-06
decay_rate = 0.95
highest = lax.Precision.HIGHEST


def shards(momentum, gradient, right_factor):
    buffer = momentum[0] + gradient[0].astype(jnp.float32)
    replicas = lax.axis_size("rep")
    columns = buffer
    partial_left = jnp.dot(
        columns,
        lax.all_gather(right_factor, "fsdp", axis=0, tiled=True),
        precision=highest,
        preferred_element_type=jnp.float32,
    )
    projected = lax.psum(partial_left, "rep")
    local_gram = jnp.dot(
        projected.T, projected, precision=highest, preferred_element_type=jnp.float32
    )
    gram_matrix = lax.psum(local_gram, "fsdp")
    lower_factor = jnp.linalg.cholesky(gram_matrix)
    orthonormal = jax.scipy.linalg.solve_triangular(lower_factor, projected.T, lower=True).T
    columns = buffer
    scattered = lax.psum_scatter(
        lax.dot_general(
            columns,
            orthonormal,
            (((0,), (0,)), ((), ())),
            precision=highest,
            preferred_element_type=jnp.float32,
        ),
        "fsdp",
        scatter_dimension=0,
        tiled=True,
    )
    own_factor = lax.psum(scattered, "rep") / replicas
    full_factor = lax.all_gather(own_factor, "fsdp", axis=0, tiled=True)
    col_norms = jnp.sqrt(jnp.sum(full_factor * full_factor, axis=0) + epsilon)
    new_factor = own_factor / col_norms
    correction = lax.dot_general(
        orthonormal,
        full_factor,
        (((1,), (1,)), ((), ())),
        precision=highest,
        preferred_element_type=jnp.float32,
    )
    new_momentum = (buffer - (1.0 - decay_rate) * correction)[None]
    direction = lax.dot_general(
        orthonormal,
        full_factor / col_norms,
        (((1,), (1,)), ((), ())),
        precision=highest,
        preferred_element_type=jnp.float32,
    )
    update = (math.sqrt(ROWS * COLS / RANK) * direction).astype(jnp.bfloat16)
    return (new_momentum, update, new_factor)


def solution(mesh):
    in_specs = (P("rep", "fsdp", None), P("rep", "fsdp", None), P("fsdp", None))
    out_specs = (P("rep", "fsdp", None), P("fsdp", None), P("fsdp", None))
    return jax.shard_map(shards, mesh=mesh, in_specs=in_specs, out_specs=out_specs, check_vma=False)
```

profile of v0, /device:TPU:0, one launch (start us, length us, event | category | flops | bytes accessed | tf_op | source)
XLA Modules:
  0.0 512.4 jit_solution(980822565762107197)
XLA Ops:
  7.2 0.7 all-gather.3.cloned.1.call-update
  7.9 35.9 %all-gather.3.cloned.1.call-done = f32[2304,256]{1,0:T(8,128)} async-done(((f32[288,256]{1,0:T(8,128)}), f32[2304,256]{1,0:T(8,128)}) %all-gather.3.cloned.1.call-update) | async-done | bytes 2359312 | tf_op jit(solution)/shard_map/all_gather | solution.py:21
  43.8 22.8 %fusion.3 = f32[2304,256]{1,0:T(8,128)} fusion(f32[2304,256]{1,0:T(8,128)} %all-gather.3.cloned.1.call-done, f32[1,2304,2304]{2,1,0:T(8,128)} %param.3, bf16[1,2304,2304]{2,1,0:T(8,128)(2,1)} %param.4), kind=kOutput, calls=%fused_computation.7 | convolution fusion | flops 16318070784 | bytes 36569088 | tf_op jit(solution)/shard_map/dot_general | solution.py:19
  66.7 73.2 %all-reduce.5.cloned.1.call-done = f32[2304,256]{1,0:T(8,128)} async-done(((f32[2304,256]{1,0:T(8,128)}), f32[2304,256]{1,0:T(8,128)}) %all-reduce.5.cloned.1.call-update) | async-done | bytes 2359312 | tf_op jit(solution)/shard_map/psum | solution.py:25
  139.9 6.9 %fusion.21 = f32[256,256]{0,1:T(8,128)} fusion(f32[2304,256]{1,0:T(8,128)} %all-reduce.5.cloned.1.call-done), kind=kOutput, calls=%fused_computation.48 | convolution fusion | flops 1811939328 | bytes 2621440 | tf_op jit(solution)/shard_map/dot_general | solution.py:26
  146.9 0.3 reduce-scatter.2.cloned.1.call-start
  147.1 55.3 %all-reduce.7.cloned.1.call-done = f32[256,256]{0,1:T(8,128)} async-done(((f32[256,256]{0,1:T(8,128)}), f32[256,256]{0,1:T(8,128)}) %all-reduce.7.cloned.1.call-update) | async-done | bytes 262160 | tf_op jit(solution)/shard_map/psum | solution.py:29
  202.4 1.1 copy.7
  203.5 1.0 fusion.11
  204.5 11.7 %cholesky.50 = f32[128,128]{1,0:T(8,128)S(1)} custom-call(f32[128,128]{1,0:T(8,128)S(1)} %cholesky.118), custom_call_target="Cholesky" | custom-call | tf_op jit(solution)/shard_map/jit(cholesky)/cholesky | solution.py:30
  216.3 9.8 %custom-call.15 = f32[1,128,128]{1,2,0:T(8,128)S(1)} custom-call(f32[1,128,128]{2,1,0:T(8,128)S(1)} %get-tuple-element.24), custom_call_target="InvertDiagBlocksLowerTriangular" | custom-call | tf_op jit(solution)/shard_map/jit(cholesky)/cholesky | solution.py:30
  226.3 0.3 convolution_subtract_fusion.1
  226.6 11.7 %cholesky.105 = f32[128,128]{1,0:T(8,128)S(1)} custom-call(f32[128,128]{1,0:T(8,128)S(1)} %convolution_subtract_fusion.1), custom_call_target="Cholesky" | custom-call | tf_op jit(solution)/shard_map/jit(cholesky)/cholesky | solution.py:30
  238.3 0.6 compare_reduce_fusion
  240.4 4.4 while.1
  240.8 0.6 fusion.31
  241.4 1.4 bitcast_dynamic-update-slice_fusion.2
  242.8 0.6 fusion.31
  243.4 1.4 bitcast_dynamic-update-slice_fusion.2
  244.8 20.3 %custom-call.16 = f32[2,128,128]{1,2,0:T(8,128)} custom-call(f32[2,128,128]{2,1,0:T(8,128)S(1)} %get-tuple-element.10), custom_call_target="InvertDiagBlocksLowerTriangular" | custom-call | tf_op jit(solution)/shard_map/jit(_solve_triangular)/triangular_solve | solution.py:31
  265.1 2.0 fusion.8
  267.1 2.9 convolution_subtract_fusion
  270.0 1.2 fusion.13
  271.2 38.5 %fusion.1 = f32[2304,256]{1,0:T(8,128)} fusion(f32[1,2304,2304]{2,1,0:T(8,128)} %param.3, bf16[1,2304,2304]{2,1,0:T(8,128)(2,1)} %param.4, f32[128,2304]{1,0:T(8,128)S(1)} %fusion.13, f32[128,2304]{1,0:T(8,128)S(1)} %fusion.8), kind=kOutput, calls=%fused_computation.5 | convolution fusion | flops 16318660608 | bytes 36569088 | tf_op jit(solution)/shard_map/dot_general | solution.py:34
  309.7 36.2 %reduce-scatter.2.cloned.1.call-done = f32[288,256]{1,0:T(8,128)} async-done(((f32[2304,256]{1,0:T(8,128)}), f32[288,256]{1,0:T(8,128)}) %reduce-scatter.2.cloned.1.call-update) | async-done | bytes 294928 | tf_op jit(solution)/shard_map/reduce_scatter | solution.py:33
  346.0 45.0 %all-reduce.9.cloned.1.call-done = f32[288,256]{1,0:T(8,128)} async-done(((f32[288,256]{1,0:T(8,128)}), f32[288,256]{1,0:T(8,128)}) %all-reduce.9.cloned.1.call-update) | async-done | bytes 294928 | tf_op jit(solution)/shard_map/psum | solution.py:45
  391.0 1.8 broadcast_multiply_fusion
  392.8 31.8 %all-gather.5.cloned.1.call-done = f32[2304,256]{1,0:T(8,128)} async-done(((f32[288,256]{1,0:T(8,128)}), f32[2304,256]{1,0:T(8,128)}) %all-gather.5.cloned.1.call-update) | async-done | bytes 2359312 | tf_op jit(solution)/shard_map/all_gather | solution.py:46
  424.5 2.1 multiply_reduce_fusion
  426.7 0.7 broadcast_divide_fusion
  427.4 36.8 %fusion.6 = bf16[2304,2304]{1,0:T(8,128)(2,1)} fusion(f32[2304,256]{1,0:T(8,128)} %all-gather.5.cloned.1.call-done, f32[128,2304]{1,0:T(8,128)S(1)} %fusion.13, f32[128,2304]{1,0:T(8,128)S(1)} %fusion.8, f32[256]{0:T(256)S(1)} %add_sqrt_fusion), kind=kOutput, calls=%fused_computation.11 | convolution fusion | flops 16319250432 | bytes 15336448 | tf_op jit(solution)/shard_map/dot_general | solution.py:57
  464.3 40.8 %fusion.5 = f32[1,2304,2304]{2,1,0:T(8,128)} fusion(f32[2304,256]{1,0:T(8,128)} %all-gather.5.cloned.1.call-done, f32[1,2304,2304]{2,1,0:T(8,128)} %param.3, bf16[1,2304,2304]{2,1,0:T(8,128)(2,1)S(1)} %bitcast.47, f32[128,2304]{1,0:T(8,128)S(1)} %fusion.13, f32[128,2304]{1,0:T(8,128)S(1)} %fusion.8), kind=kOutput, calls=%fused_computation.10 | convolution fusion | flops 16329277440 | bytes 57802752 | tf_op jit(solution)/shard_map/dot_general | solution.py:49
  (37 shorter events, 0.7 us)
Async XLA Ops:
  7.2 36.6 %all-gather.3.cloned.1.call-start = ((), (), s32[]{:S(2)}) async-start(), calls=%async_computation.1 | async-start | bytes 2654208 | tf_op jit(solution)/shard_map/all_gather | solution.py:21
  7.9 132.0 %all-reduce.5.cloned.1.call-start = ((), (), s32[]{:S(2)}) async-start(), calls=%async_computation.2 | async-start | bytes 4718592 | tf_op jit(solution)/shard_map/psum | solution.py:25
  66.6 135.8 %all-reduce.7.cloned.1.call-start = ((), (), s32[]{:S(2)}) async-start(), calls=%async_computation.3 | async-start | bytes 524288 | tf_op jit(solution)/shard_map/psum | solution.py:29
  146.8 118.3 %copy-start = (f32[2304,256]{1,0:T(8,128)S(1)}, f32[2304,256]{1,0:T(8,128)}, u32[]{:S(2)}) copy-start(f32[2304,256]{1,0:T(8,128)} %all-reduce.5.cloned.1.call-done) | copy-start | bytes 7077892
  146.9 199.1 %reduce-scatter.2.cloned.1.call-start = ((), (), s32[]{:S(2)}) async-start(), calls=%async_computation.4 | async-start | bytes 2654208 | tf_op jit(solution)/shard_map/reduce_scatter | solution.py:33
  244.8 20.3 %copy-start.1 = (f32[256,256]{1,0:T(8,128)}, f32[256,256]{1,0:T(8,128)S(1)}, u32[]{:S(2)}) copy-start(f32[256,256]{1,0:T(8,128)S(1)} %get-tuple-element.86) | copy-start | bytes 786436
  267.1 2.9 copy-start.3
  309.7 81.3 %all-reduce.9.cloned.1.call-start = ((), (), s32[]{:S(2)}) async-start(), calls=%async_computation.5 | async-start | bytes 589824 | tf_op jit(solution)/shard_map/psum | solution.py:45
  346.0 78.6 %all-gather.5.cloned.1.call-start = ((), (), s32[]{:S(2)}) async-start(), calls=%async_computation.6 | async-start | bytes 2654208 | tf_op jit(solution)/shard_map/all_gather | solution.py:46
  391.0 35.7 %copy-start.2 = (f32[288,256]{1,0:T(8,128)S(1)}, f32[288,256]{1,0:T(8,128)}, u32[]{:S(2)}) copy-start(f32[288,256]{1,0:T(8,128)} %all-reduce.9.cloned.1.call-done) | copy-start | bytes 884740
  424.5 39.7 %slice-start = ((s8[10616832]{0:T(1024)(128)(4,1)}), s8[4194304]{0:T(1024)(128)(4,1)S(1)}, s32[]{:S(2)}) async-start(s8[10616832]{0:T(1024)(128)(4,1)} %bitcast.46), calls=%async_computation.7 | async-start | bytes 8388608
  427.4 36.8 %slice-start.1 = ((s8[10616832]{0:T(1024)(128)(4,1)}), s8[4194304]{0:T(1024)(128)(4,1)S(1)}, s32[]{:S(2)}) async-start(s8[10616832]{0:T(1024)(128)(4,1)} %bitcast.46), calls=%async_computation.8 | async-start | bytes 8388608
  427.4 36.8 %slice-start.2 = ((s8[10616832]{0:T(1024)(128)(4,1)}), s8[2228224]{0:T(1024)(128)(4,1)S(1)}, s32[]{:S(2)}) async-start(s8[10616832]{0:T(1024)(128)(4,1)} %bitcast.46), calls=%async_computation.9 | async-start | bytes 4456448
Sparse Core Ops, SparseCore 0:
  9.6 34.1 all-gather.2
  66.8 73.0 all-reduce.4
  147.0 55.4 all-reduce.6
  309.8 36.0 reduce-scatter.1
  348.7 42.2 all-reduce.8
  393.1 31.4 all-gather.4
where the time goes:
time: 520 us; the launch traced here: 512 us
  waiting for transfers between devices  278 us (53%)
  matrix products  152 us (29%)
  other arithmetic  59.9 us (12%)
  between operations  16 us (3%)
    psum x1, waiting for transfers between devices, shards(): projected = lax.psum(partial_left, 'rep')  73.2 us
    psum x1, waiting for transfers between devices, shards(): gram_matrix = lax.psum(local_gram, 'fsdp')  55.3 us
    psum x1, waiting for transfers between devices, shards(): own_factor = lax.psum(scattered, 'rep') / replicas  45 us
    dot_general x1, matrix products, shards(): lax.dot_general(orthonormal, full_factor, (((1,), (1,)), ((), ())), preci...  40.8 us
    dot_general x1, matrix products, shards(): lax.dot_general(columns, orthonormal, (((0,), (0,)), ((), ())), precision...  38.5 us
    dot_general x1, matrix products, shards(): lax.dot_general(orthonormal, full_factor / col_norms, (((1,), (1,)), ((),...  36.8 us
    reduce_scatter x1, waiting for transfers between devices, shards(): lax.psum_scatter(lax.dot_general(columns, orthonormal, (((0,), (0,)), (()...  36.2 us
    all_gather x1, waiting for transfers between devices, shards(): lax.all_gather(right_factor, 'fsdp', axis=0, tiled=True)  35.9 us
  transfers between devices with their start and end apart: 6, of which 6 were waited for; matrix products, arithmetic and copies ran while one was open for 0% of the time, Pallas kernels for 0%

commit v1 on v0

--- a/solution.py
+++ b/solution.py
@@ -26,7 +26,7 @@
     local_gram = jnp.dot(
         projected.T, projected, precision=highest, preferred_element_type=jnp.float32
     )
-    gram_matrix = lax.psum(local_gram, "fsdp")
+    gram_matrix = jnp.sum(lax.all_gather(local_gram, "fsdp"), axis=0)
     lower_factor = jnp.linalg.cholesky(gram_matrix)
     orthonormal = jax.scipy.linalg.solve_triangular(lower_factor, projected.T, lower=True).T
     columns = buffer

time: 520 us -> 494 us (0.950)
  waiting for transfers between devices: 278 us -> 252 us
    psum x1 -> x0, waiting for transfers between devices: 55.3 us -> none  [shards(): gram_matrix = lax.psum(local_gram, 'fsdp')]
    all_gather x0 -> x1, waiting for transfers between devices: none -> 29 us  [shards(): gram_matrix = jnp.sum(lax.all_gather(local_gram, 'fsdp'), axis=0)]
where the time goes in v1:
time: 494 us; the launch traced here: 486 us
  waiting for transfers between devices  252 us (51%)
  matrix products  152 us (31%)
  other arithmetic  60.7 us (12%)
  between operations  16 us (3%)
    psum x1, waiting for transfers between devices, shards(): projected = lax.psum(partial_left, 'rep')  73.2 us
    psum x1, waiting for transfers between devices, shards(): own_factor = lax.psum(scattered, 'rep') / replicas  45 us
    dot_general x1, matrix products, shards(): lax.dot_general(orthonormal, full_factor, (((1,), (1,)), ((), ())), preci...  40.8 us
    dot_general x1, matrix products, shards(): lax.dot_general(columns, orthonormal, (((0,), (0,)), ((), ())), precision...  38.5 us
    dot_general x1, matrix products, shards(): lax.dot_general(orthonormal, full_factor / col_norms, (((1,), (1,)), ((),...  36.8 us
    reduce_scatter x1, waiting for transfers between devices, shards(): lax.psum_scatter(lax.dot_general(columns, orthonormal, (((0,), (0,)), (()...  36.6 us
    all_gather x1, waiting for transfers between devices, shards(): lax.all_gather(right_factor, 'fsdp', axis=0, tiled=True)  35.9 us
    another operation x6, other arithmetic, shards(): lower_factor = jnp.linalg.cholesky(gram_matrix)  33.9 us
  transfers between devices with their start and end apart: 6, of which 6 were waited for; matrix products, arithmetic and copies ran while one was open for 0% of the time, Pallas kernels for 0%

profile of v1, /device:TPU:0, one launch (start us, length us, event | category | flops | bytes accessed | tf_op | source)
XLA Modules:
  0.0 486.4 jit_solution(8685304740107629261)
XLA Ops:
  7.2 0.7 all-gather.5.cloned.1.call-update
  7.9 35.9 %all-gather.5.cloned.1.call-done = f32[2304,256]{1,0:T(8,128)} async-done(((f32[288,256]{1,0:T(8,128)}), f32[2304,256]{1,0:T(8,128)}) %all-gather.5.cloned.1.call-update) | async-done | bytes 2359312 | tf_op jit(solution)/shard_map/all_gather | solution.py:21
  43.8 22.8 %fusion.3 = f32[2304,256]{1,0:T(8,128)} fusion(f32[2304,256]{1,0:T(8,128)} %all-gather.5.cloned.1.call-done, f32[1,2304,2304]{2,1,0:T(8,128)} %param.3, bf16[1,2304,2304]{2,1,0:T(8,128)(2,1)} %param.4), kind=kOutput, calls=%fused_computation.7 | convolution fusion | flops 16318070784 | bytes 36569088 | tf_op jit(solution)/shard_map/dot_general | solution.py:19
  66.7 73.2 %all-reduce.4.cloned.1.call-done = f32[2304,256]{1,0:T(8,128)} async-done(((f32[2304,256]{1,0:T(8,128)}), f32[2304,256]{1,0:T(8,128)}) %all-reduce.4.cloned.1.call-update) | async-done | bytes 2359312 | tf_op jit(solution)/shard_map/psum | solution.py:25
  139.9 7.0 %fusion.21 = f32[256,256]{1,0:T(8,128)} fusion(f32[2304,256]{1,0:T(8,128)} %all-reduce.4.cloned.1.call-done), kind=kOutput, calls=%fused_computation.48 | convolution fusion | flops 1811939328 | bytes 2621440 | tf_op jit(solution)/shard_map/dot_general | solution.py:26
  146.9 0.3 reduce-scatter.2.cloned.1.call-start
  147.2 29.0 %all-gather.9.cloned.1.call-done = f32[2048,256]{1,0:T(8,128)} async-done(((f32[256,256]{1,0:T(8,128)}), f32[2048,256]{1,0:T(8,128)}) %all-gather.9.cloned.1.call-update) | async-done | bytes 2097168 | tf_op jit(solution)/shard_map/all_gather | solution.py:29
  176.2 1.8 reduce_sum.18
  178.1 11.7 %cholesky.50 = f32[128,128]{1,0:T(8,128)S(1)} custom-call(f32[128,128]{1,0:T(8,128)S(1)} %cholesky.118), custom_call_target="Cholesky" | custom-call | tf_op jit(solution)/shard_map/jit(cholesky)/cholesky | solution.py:30
  189.9 9.8 %custom-call.15 = f32[1,128,128]{1,2,0:T(8,128)S(1)} custom-call(f32[1,128,128]{2,1,0:T(8,128)S(1)} %get-tuple-element.24), custom_call_target="InvertDiagBlocksLowerTriangular" | custom-call | tf_op jit(solution)/shard_map/jit(cholesky)/cholesky | solution.py:30
  199.7 0.2 constant_dynamic-update-slice_fusion.1
  199.9 0.3 convolution_subtract_fusion.1
  200.2 11.7 %cholesky.105 = f32[128,128]{1,0:T(8,128)S(1)} custom-call(f32[128,128]{1,0:T(8,128)S(1)} %convolution_subtract_fusion.1), custom_call_target="Cholesky" | custom-call | tf_op jit(solution)/shard_map/jit(cholesky)/cholesky | solution.py:30
  212.0 0.6 compare_reduce_fusion
  214.0 4.4 while.1
  214.4 0.6 fusion.31
  215.0 1.4 bitcast_dynamic-update-slice_fusion.2
  216.4 0.6 fusion.31
  217.0 1.4 bitcast_dynamic-update-slice_fusion.2
  218.4 20.3 %custom-call.16 = f32[2,128,128]{1,2,0:T(8,128)} custom-call(f32[2,128,128]{2,1,0:T(8,128)S(1)} %get-tuple-element.10), custom_call_target="InvertDiagBlocksLowerTriangular" | custom-call | tf_op jit(solution)/shard_map/jit(_solve_triangular)/triangular_solve | solution.py:31
  238.7 2.0 fusion.8
  240.8 2.9 convolution_subtract_fusion
  243.7 1.2 fusion.13
  244.8 38.5 %fusion.1 = f32[2304,256]{1,0:T(8,128)} fusion(f32[1,2304,2304]{2,1,0:T(8,128)} %param.3, bf16[1,2304,2304]{2,1,0:T(8,128)(2,1)} %param.4, f32[128,2304]{1,0:T(8,128)S(1)} %fusion.13, f32[128,2304]{1,0:T(8,128)S(1)} %fusion.8), kind=kOutput, calls=%fused_computation.5 | convolution fusion | flops 16318660608 | bytes 36569088 | tf_op jit(solution)/shard_map/dot_general | solution.py:34
  283.4 36.6 %reduce-scatter.2.cloned.1.call-done = f32[288,256]{1,0:T(8,128)} async-done(((f32[2304,256]{1,0:T(8,128)}), f32[288,256]{1,0:T(8,128)}) %reduce-scatter.2.cloned.1.call-update) | async-done | bytes 294928 | tf_op jit(solution)/shard_map/reduce_scatter | solution.py:33
  320.0 45.0 %all-reduce.6.cloned.1.call-done = f32[288,256]{1,0:T(8,128)} async-done(((f32[288,256]{1,0:T(8,128)}), f32[288,256]{1,0:T(8,128)}) %all-reduce.6.cloned.1.call-update) | async-done | bytes 294928 | tf_op jit(solution)/shard_map/psum | solution.py:45
  365.0 1.8 broadcast_multiply_fusion
  366.8 31.8 %all-gather.7.cloned.1.call-done = f32[2304,256]{1,0:T(8,128)} async-done(((f32[288,256]{1,0:T(8,128)}), f32[2304,256]{1,0:T(8,128)}) %all-gather.7.cloned.1.call-update) | async-done | bytes 2359312 | tf_op jit(solution)/shard_map/all_gather | solution.py:46
  398.6 2.1 multiply_reduce_fusion
  400.7 0.7 broadcast_divide_fusion
  401.5 36.8 %fusion.6 = bf16[2304,2304]{1,0:T(8,128)(2,1)} fusion(f32[2304,256]{1,0:T(8,128)} %all-gather.7.cloned.1.call-done, f32[128,2304]{1,0:T(8,128)S(1)} %fusion.13, f32[128,2304]{1,0:T(8,128)S(1)} %fusion.8, f32[256]{0:T(256)S(1)} %add_sqrt_fusion), kind=kOutput, calls=%fused_computation.11 | convolution fusion | flops 16319250432 | bytes 15336448 | tf_op jit(solution)/shard_map/dot_general | solution.py:57
  438.3 40.8 %fusion.5 = f32[1,2304,2304]{2,1,0:T(8,128)} fusion(f32[2304,256]{1,0:T(8,128)} %all-gather.7.cloned.1.call-done, f32[1,2304,2304]{2,1,0:T(8,128)} %param.3, bf16[1,2304,2304]{2,1,0:T(8,128)(2,1)S(1)} %bitcast.48, f32[128,2304]{1,0:T(8,128)S(1)} %fusion.13, f32[128,2304]{1,0:T(8,128)S(1)} %fusion.8), kind=kOutput, calls=%fused_computation.10 | convolution fusion | flops 16329277440 | bytes 57802752 | tf_op jit(solution)/shard_map/dot_general | solution.py:49
  (38 shorter events, 0.7 us)
Async XLA Ops:
  7.2 36.6 %all-gather.5.cloned.1.call-start = ((), (), s32[]{:S(2)}) async-start(), calls=%async_computation.1 | async-start | bytes 2654208 | tf_op jit(solution)/shard_map/all_gather | solution.py:21
  7.9 132.0 %all-reduce.4.cloned.1.call-start = ((), (), s32[]{:S(2)}) async-start(), calls=%async_computation.2 | async-start | bytes 4718592 | tf_op jit(solution)/shard_map/psum | solution.py:25
  66.6 109.5 %all-gather.9.cloned.1.call-start = ((), (), s32[]{:S(2)}) async-start(), calls=%async_computation.6 | async-start | bytes 2359296 | tf_op jit(solution)/shard_map/all_gather | solution.py:29
  146.9 173.1 %reduce-scatter.2.cloned.1.call-start = ((), (), s32[]{:S(2)}) async-start(), calls=%async_computation.3 | async-start | bytes 2654208 | tf_op jit(solution)/shard_map/reduce_scatter | solution.py:33
  177.9 60.8 %copy-start = (f32[2304,256]{1,0:T(8,128)S(1)}, f32[2304,256]{1,0:T(8,128)}, u32[]{:S(2)}) copy-start(f32[2304,256]{1,0:T(8,128)} %all-reduce.4.cloned.1.call-done) | copy-start | bytes 7077892
  218.4 20.3 %copy-start.1 = (f32[256,256]{1,0:T(8,128)}, f32[256,256]{1,0:T(8,128)S(1)}, u32[]{:S(2)}) copy-start(f32[256,256]{1,0:T(8,128)S(1)} %get-tuple-element.87) | copy-start | bytes 786436
  240.7 2.9 copy-start.3
  283.3 81.7 %all-reduce.6.cloned.1.call-start = ((), (), s32[]{:S(2)}) async-start(), calls=%async_computation.4 | async-start | bytes 589824 | tf_op jit(solution)/shard_map/psum | solution.py:45
  320.0 78.6 %all-gather.7.cloned.1.call-start = ((), (), s32[]{:S(2)}) async-start(), calls=%async_computation.5 | async-start | bytes 2654208 | tf_op jit(solution)/shard_map/all_gather | solution.py:46
  365.0 35.7 %copy-start.2 = (f32[288,256]{1,0:T(8,128)S(1)}, f32[288,256]{1,0:T(8,128)}, u32[]{:S(2)}) copy-start(f32[288,256]{1,0:T(8,128)} %all-reduce.6.cloned.1.call-done) | copy-start | bytes 884740
  398.6 39.7 %slice-start = ((s8[10616832]{0:T(1024)(128)(4,1)}), s8[4194304]{0:T(1024)(128)(4,1)S(1)}, s32[]{:S(2)}) async-start(s8[10616832]{0:T(1024)(128)(4,1)} %bitcast.47), calls=%async_computation.7 | async-start | bytes 8388608
  401.5 36.8 %slice-start.1 = ((s8[10616832]{0:T(1024)(128)(4,1)}), s8[4194304]{0:T(1024)(128)(4,1)S(1)}, s32[]{:S(2)}) async-start(s8[10616832]{0:T(1024)(128)(4,1)} %bitcast.47), calls=%async_computation.8 | async-start | bytes 8388608
  401.5 36.8 %slice-start.2 = ((s8[10616832]{0:T(1024)(128)(4,1)}), s8[2228224]{0:T(1024)(128)(4,1)S(1)}, s32[]{:S(2)}) async-start(s8[10616832]{0:T(1024)(128)(4,1)} %bitcast.47), calls=%async_computation.9 | async-start | bytes 4456448
Sparse Core Ops, SparseCore 0:
  9.6 34.1 all-gather.4
  66.8 73.0 all-reduce.3
  147.0 29.1 all-gather.8
  283.4 36.4 reduce-scatter.1
  322.7 42.2 all-reduce.5
  367.1 31.4 all-gather.6
